TPU v7x, 32 devices: a whole 2x2x4 slice. The times are simulated.
32 devices in a mesh: batch: 4 (over y, x), feat: 8 (over z, core).
Axes of the slice: x: 2, y: 2, z: 4, core: 2. Of those that a mesh axis runs over, the one named last changes fastest.
Arguments:
- view_a: bfloat16 [1024, 8192], P('batch', 'feat'), may hold values from -16 to 16
- view_b: bfloat16 [1024, 8192], P('batch', 'feat'), may hold values from -16 to 16
Outputs:
- loss_value: float32 [], replicated
- grad_a: float32 [1024, 8192], P('batch', 'feat')
- grad_b: float32 [1024, 8192], P('batch', 'feat')
All inputs are finite; a program needn't handle non-finite values.
Results may differ from a plain program's by a relative error of at most 0.0026.
Values may be sent and summed in bfloat16 or wider, within the bound.
A program may use at most 64 MiB of HBM per device.

v0:
```python
import jax
import jax.numpy as jnp
from jax import lax
from jax.sharding import PartitionSpec as P

variance_floor = 0.25
redundancy = 0.0051


def local(view_a, view_b):
    rows_dev, cols_dev = view_a.shape
    batch_total = rows_dev * lax.axis_size("batch")
    values_a = view_a.astype(jnp.float32)
    values_b = view_b.astype(jnp.float32)
    totals = lax.psum((jnp.sum(values_a, axis=0), jnp.sum(values_b, axis=0)), "batch")
    shifted_a = values_a - totals[0] / batch_total
    shifted_b = values_b - totals[1] / batch_total
    squares = lax.psum(
        (jnp.sum(shifted_a * shifted_a, axis=0), jnp.sum(shifted_b * shifted_b, axis=0)), "batch"
    )
    var_a = squares[0] / batch_total
    var_b = squares[1] / batch_total
    factor_a = lax.rsqrt(var_a + variance_floor)
    factor_b = lax.rsqrt(var_b + variance_floor)
    normed_a = shifted_a * factor_a
    normed_b = shifted_b * factor_b
    low_a = normed_a.astype(jnp.bfloat16)
    low_b = normed_b.astype(jnp.bfloat16)
    whole_a = lax.all_gather(low_a, "feat", axis=1, tiled=True)
    feature_total = whole_a.shape[1]
    row_share = feature_total // lax.axis_size("batch")
    group_index = lax.axis_index("batch")
    owner_index = lax.axis_index("feat")
    slab_rows = lax.all_to_all(whole_a, "batch", split_axis=1, concat_axis=0, tiled=True)
    samples = lax.all_gather(low_b, "batch", axis=0, tiled=True)
    summed = lax.dot_general(
        slab_rows, samples, (((0,), (0,)), ((), ())), preferred_element_type=jnp.float32
    )
    cross_block = summed / batch_total
    row_ids = group_index * row_share + jnp.arange(row_share, dtype=jnp.int32)
    col_ids = owner_index * cols_dev + jnp.arange(cols_dev, dtype=jnp.int32)
    diagonal_mask = row_ids[:, None] == col_ids[None, :]
    missing = 1.0 - cross_block
    local_loss = jnp.sum(
        jnp.where(diagonal_mask, missing * missing, redundancy * cross_block * cross_block)
    )
    dcross = jnp.where(
        diagonal_mask, 2.0 * (cross_block - 1.0), 2.0 * redundancy * cross_block
    ).astype(jnp.bfloat16)
    column = lax.all_gather(dcross, "batch", axis=0, tiled=True)
    dnorm_b = jnp.dot(whole_a, column, preferred_element_type=jnp.float32)
    dnorm_a = lax.psum_scatter(
        lax.dot_general(
            column, low_b, (((1,), (1,)), ((), ())), preferred_element_type=jnp.float32
        ),
        "feat",
        scatter_dimension=0,
        tiled=True,
    ).T
    loss_value = lax.psum(local_loss, ("batch", "feat")) / feature_total
    grad_totals = lax.psum(
        (
            jnp.sum(dnorm_a, axis=0),
            jnp.sum(dnorm_a * normed_a, axis=0),
            jnp.sum(dnorm_b, axis=0),
            jnp.sum(dnorm_b * normed_b, axis=0),
        ),
        "batch",
    )
    grad_a = (
        dnorm_a - grad_totals[0] / batch_total - normed_a * (grad_totals[1] / batch_total)
    ) * factor_a
    grad_b = (
        dnorm_b - grad_totals[2] / batch_total - normed_b * (grad_totals[3] / batch_total)
    ) * factor_b
    return (loss_value, grad_a, grad_b)


def solution(mesh):
    return jax.shard_map(
        local,
        mesh=mesh,
        in_specs=(P("batch", "feat"), P("batch", "feat")),
        out_specs=(P(), P("batch", "feat"), P("batch", "feat")),
        check_vma=False,
    )
```

profile of v0, /device:TPU:0, one launch (start us, length us, event | category | flops | bytes accessed | tf_op | source)
XLA Modules:
  0.0 459.0 jit_solution(14359632467602067935)
XLA Ops:
  7.2 0.0 all-gather.4.cloned.1.call-start
  7.2 1.1 convert_reduce_fusion
  8.3 1.2 copy.7
  9.6 0.2 convert_reduce_fusion.1
  9.8 11.5 %all-reduce.2 = (f32[1024]{0:T(1024)S(1)}, f32[1024]{0:T(1024)S(1)}) all-reduce(f32[1024]{0:T(1024)S(1)} %convert_reduce_fusion.1, f32[1024]{0:T(1024)S(1)} %convert_reduce_fusion), channel_id=1, replica_groups=mesh['batch'=4,'feat'=8] {'batch'}, use_global_device_ids=true, to_apply=%region_1.0 | all-reduce | flops 2048 | bytes 16384 | tf_op jit(solution)/shard_map/psum | solution.py:15
  21.4 1.2 fusion.15
  22.6 0.4 fusion.19
  22.9 8.2 %all-reduce.1 = (f32[1024]{0:T(1024)S(1)}, f32[1024]{0:T(1024)S(1)}) all-reduce(f32[1024]{0:T(1024)S(1)} %fusion.19, f32[1024]{0:T(1024)S(1)} %fusion.15), channel_id=1, replica_groups=mesh['batch'=4,'feat'=8] {'batch'}, use_global_device_ids=true, to_apply=%region_3.0 | all-reduce | flops 2048 | bytes 16384 | tf_op jit(solution)/shard_map/psum | solution.py:18
  31.1 1.1 fusion.6
  32.3 0.0 all-gather.4.cloned.1.call-update
  32.3 0.0 all-gather.6.cloned.1.call-start
  32.3 2.0 fusion.11
  34.3 0.0 all-gather.6.cloned.1.call-update
  34.3 45.2 %all-gather.4.cloned.1.call-done = bf16[256,8192]{0,1:T(8,128)(2,1)} async-done(((bf16[256,1024]{0,1:T(8,128)(2,1)}), bf16[256,8192]{0,1:T(8,128)(2,1)}) %all-gather.4.cloned.1.call-update) | async-done | bytes 4194320 | tf_op jit(solution)/shard_map/all_gather | solution.py:29
  79.6 6.4 %copy.8 = bf16[256,4,2048]{2,0,1:T(8,128)(2,1)} copy(bf16[256,4,2048]{0,2,1:T(8,128)(2,1)} %bitcast.15) | data formatting | bytes 8388608 | tf_op jit(solution)/shard_map/all_to_all | solution.py:34
  86.0 4.9 %all-to-all-start = ((bf16[256,4,2048]{2,0,1:T(8,128)(2,1)}), bf16[256,4,2048]{2,0,1:T(8,128)(2,1)}, u32[]{:S(2)}, u32[]{:S(2)}) async-start(bf16[256,4,2048]{2,0,1:T(8,128)(2,1)} %copy.8), calls=%async_computation | async-start | bytes 8388608 | tf_op jit(solution)/shard_map/all_to_all | solution.py:34
  90.9 0.0 all-gather.8.cloned.1.call-start
  91.0 62.4 %all-gather.6.cloned.1.call-done = bf16[1024,1024]{1,0:T(8,128)(2,1)} async-done(((bf16[256,1024]{1,0:T(8,128)(2,1)}), bf16[1024,1024]{1,0:T(8,128)(2,1)}) %all-gather.6.cloned.1.call-update) | async-done | bytes 2097168 | tf_op jit(solution)/shard_map/all_gather | solution.py:35
  153.4 0.0 all-to-all-done
  153.4 0.0 copy-start.1
  153.4 12.6 %fusion.1 = (bf16[2048,1024]{1,0:T(8,128)(2,1)}, f32[]{:T(128)}) fusion(s32[1024]{0:T(1024)S(1)} %iota_add_fusion.1, s32[2048]{0:T(1024)S(1)} %iota_add_fusion, bf16[1024,2048]{1,0:T(8,128)(2,1)} %bitcast.2, bf16[1024,1024]{1,0:T(8,128)(2,1)} %all-gather.6.cloned.1.call-done), kind=kOutput, calls=%fused_computation.3 | convolution fusion | flops 4322230272 | bytes 10498052 | tf_op jit(solution)/shard_map/dot_general | solution.py:36
  166.0 0.0 all-gather.8.cloned.1.call-update
  166.0 0.0 reduce-scatter.2.cloned.1.call-start
  166.1 157.4 %all-gather.8.cloned.1.call-done = bf16[8192,1024]{1,0:T(8,128)(2,1)} async-done(((bf16[2048,1024]{1,0:T(8,128)(2,1)}), bf16[8192,1024]{1,0:T(8,128)(2,1)}) %all-gather.8.cloned.1.call-update) | async-done | bytes 16777232 | tf_op jit(solution)/shard_map/all_gather | solution.py:50
  323.5 0.0 copy-done.1
  323.5 13.6 %fusion.21 = f32[8192,256]{1,0:T(8,128)} fusion(bf16[8192,1024]{1,0:T(8,128)(2,1)} %all-gather.8.cloned.1.call-done, bf16[256,1024]{1,0:T(8,128)(2,1)S(1)} %copy-done.1), kind=kOutput, calls=%fused_computation.38 | convolution fusion | flops 4294967296 | bytes 25690112 | tf_op jit(solution)/shard_map/dot_general | solution.py:53
  337.0 0.0 copy-start
  337.0 0.0 reduce-scatter.2.cloned.1.call-update
  337.1 41.3 %psum.67 = f32[]{:T(128)} all-reduce(f32[]{:T(128)} %get-tuple-element.20), channel_id=1, replica_groups=mesh['batch'=4,'feat'=8] {'batch','feat'}, use_global_device_ids=true, to_apply=%region_9.10 | all-reduce | flops 1 | bytes 8 | tf_op jit(solution)/shard_map/psum | solution.py:60
  379.0 0.0 copy-done
  379.0 9.6 %fusion.20 = (f32[1024]{0:T(1024)S(1)}, f32[1024]{0:T(1024)S(1)}, f32[256,1024]{1,0:T(8,128)S(1)}) fusion(f32[1024]{0:T(1024)S(1)} %add_rsqrt_fusion, f32[1024]{0:T(1024)S(1)} %get-tuple-element.22, bf16[256,1024]{1,0:T(8,128)(2,1)S(1)} %copy-done, bf16[256,8192]{0,1:T(8,128)(2,1)} %all-gather.4.cloned.1.call-done, ...), kind=kOutput, calls=%fused_computation.37 | convolution fusion | flops 4296538112 | bytes 22560768 | tf_op jit(solution)/shard_map/dot_general | solution.py:51
  388.6 39.2 %reduce-scatter.2.cloned.1.call-done = f32[1024,256]{1,0:T(8,128)} async-done(((f32[8192,256]{1,0:T(8,128)}), f32[1024,256]{1,0:T(8,128)}) %reduce-scatter.2.cloned.1.call-update) | async-done | bytes 1048592 | tf_op jit(solution)/shard_map/reduce_scatter | solution.py:52
  427.8 1.7 fusion.16
  429.5 1.4 reduce_sum.86
  431.0 15.9 %all-reduce = (f32[1024]{0:T(1024)S(1)}, f32[1024]{0:T(1024)S(1)}, f32[1024]{0:T(1024)S(1)}, f32[1024]{0:T(1024)S(1)}) all-reduce(f32[1024]{0:T(1024)S(1)} %fusion.16, f32[1024]{0:T(1024)S(1)} %reduce_sum.86, f32[1024]{0:T(1024)S(1)} %get-tuple-element.10, f32[1024]{0:T(1024)S(1)} %get-tuple-element.9), channel_id=1, replica_groups=mesh['batch'=4,'feat'=8] {'batch'}, use_global_device_ids=true, to_apply=%region_14.15 | all-reduce | flops 4096 | bytes 32768 | tf_op jit(solution)/shard_map/psum | solution.py:61
  446.9 1.9 fusion.18
  448.8 1.3 copy.9
  450.1 1.2 fusion.14
  (9 shorter events, 0.0 us)
Async XLA Ops:
  7.2 72.4 %all-gather.4.cloned.1.call-start = ((), (), s32[]{:S(2)}) async-start(), calls=%async_computation.2 | async-start | bytes 4718592 | tf_op jit(solution)/shard_map/all_gather | solution.py:29
  32.3 121.1 %all-gather.6.cloned.1.call-start = ((), (), s32[]{:S(2)}) async-start(), calls=%async_computation.3 | async-start | bytes 2621440 | tf_op jit(solution)/shard_map/all_gather | solution.py:35
  86.0 67.4 %all-to-all-start = ((bf16[256,4,2048]{2,0,1:T(8,128)(2,1)}), bf16[256,4,2048]{2,0,1:T(8,128)(2,1)}, u32[]{:S(2)}, u32[]{:S(2)}) async-start(bf16[256,4,2048]{2,0,1:T(8,128)(2,1)} %copy.8), calls=%async_computation | async-start | bytes 8388608 | tf_op jit(solution)/shard_map/all_to_all | solution.py:34
  90.9 232.6 %all-gather.8.cloned.1.call-start = ((), (), s32[]{:S(2)}) async-start(), calls=%async_computation.4 | async-start | bytes 20971520 | tf_op jit(solution)/shard_map/all_gather | solution.py:50
  153.4 170.1 %copy-start.1 = (bf16[256,1024]{1,0:T(8,128)(2,1)S(1)}, bf16[256,1024]{1,0:T(8,128)(2,1)}, u32[]{:S(2)}) copy-start(bf16[256,1024]{1,0:T(8,128)(2,1)} %fusion.11) | copy-start | bytes 1572868
  166.0 261.8 %reduce-scatter.2.cloned.1.call-start = ((), (), s32[]{:S(2)}) async-start(), calls=%async_computation.5 | async-start | bytes 9437184 | tf_op jit(solution)/shard_map/reduce_scatter | solution.py:52
  337.0 42.0 %copy-start = (bf16[256,1024]{1,0:T(8,128)(2,1)S(1)}, bf16[256,1024]{1,0:T(8,128)(2,1)}, u32[]{:S(2)}) copy-start(bf16[256,1024]{1,0:T(8,128)(2,1)} %param.3) | copy-start | bytes 1572868
Sparse Core Ops, SparseCore 0:
  32.4 47.1 all-gather.3
  82.0 71.3 all-gather.5
  166.1 157.2 all-gather.7
  337.2 90.5 reduce-scatter.1
where the time goes:
time: 460 us; the launch traced here: 459 us
  waiting for transfers between devices  304 us (66%)
  blocking collectives  76.9 us (17%)
  matrix products  35.8 us (8%)
  between operations  15.7 us (3%)
  other arithmetic  12.3 us (3%)
  local copies, waits for them, and re-layouts  8.95 us (2%)
  starting transfers between devices  5.07 us (1%)
    all_gather x1, waiting for transfers between devices, local(): column = lax.all_gather(dcross, 'batch', axis=0, tiled=True)  157 us
    all_gather x1, waiting for transfers between devices, local(): samples = lax.all_gather(low_b, 'batch', axis=0, tiled=True)  62.4 us
    all_gather x1, waiting for transfers between devices, local(): whole_a = lax.all_gather(low_a, 'feat', axis=1, tiled=True)  45.2 us
    psum x1, blocking collectives, local(): loss_value = lax.psum(local_loss, ('batch', 'feat')) / feature_total  41.3 us
    reduce_scatter x1, waiting for transfers between devices, local(): lax.psum_scatter(lax.dot_general(column, low_b, (((1,), (1,)), ((), ())),...  39.2 us
    psum x1, blocking collectives, local(): lax.psum((jnp.sum(dnorm_a, axis=0), jnp.sum(dnorm_a * normed_a, axis=0),...  15.9 us
    dot_general x1, matrix products, local(): lax.dot_general(column, low_b, (((1,), (1,)), ((), ())), preferred_elemen...  13.6 us
    dot_general x1, matrix products, local(): lax.dot_general(slab_rows, samples, (((0,), (0,)), ((), ())), preferred_e...  12.6 us
  transfers between devices with their start and end apart: 5, of which 4 were waited for; matrix products, arithmetic and copies ran while one was open for 4% of the time, Pallas kernels for 0%

commit v1 on v0

v1 whole, which is shorter than its diff:
```python
import jax
import jax.numpy as jnp
from jax import lax
from jax.sharding import PartitionSpec as P

variance_floor = 0.25
redundancy = 0.0051


def local(view_a, view_b):
    rows_dev, cols_dev = view_a.shape
    groups = lax.axis_size("batch")
    batch_total = rows_dev * groups
    feature_total = cols_dev * lax.axis_size("feat")
    scale = 2.0 * redundancy / batch_total
    all_a = lax.all_gather(view_a, "batch", axis=0, tiled=True).astype(jnp.float32)
    all_b = lax.all_gather(view_b, "batch", axis=0, tiled=True).astype(jnp.float32)

    def normalize(values):
        shifted = values - jnp.mean(values, axis=0)
        factor = lax.rsqrt(jnp.mean(shifted * shifted, axis=0) + variance_floor)
        return shifted * factor, factor

    full_a, factor_a = normalize(all_a)
    full_b, factor_b = normalize(all_b)
    samples_a = full_a.astype(jnp.bfloat16)
    samples_b = full_b.astype(jnp.bfloat16)
    start = lax.axis_index("batch") * rows_dev
    normed_a = lax.dynamic_slice_in_dim(full_a, start, rows_dev)
    normed_b = lax.dynamic_slice_in_dim(full_b, start, rows_dev)
    low_a = normed_a.astype(jnp.bfloat16)
    low_b = normed_b.astype(jnp.bfloat16)
    diagonal = (
        jnp.sum(samples_a.astype(jnp.float32) * samples_b.astype(jnp.float32), axis=0)
        / batch_total
    )
    rows_t = (((1,), (1,)), ((), ()))
    gram_a = lax.dot_general(low_a, samples_a, rows_t, preferred_element_type=jnp.float32)
    gram_b = lax.dot_general(low_b, samples_b, rows_t, preferred_element_type=jnp.float32)
    gram_a, gram_b = lax.psum((gram_a, gram_b), "feat")
    square_sum = jnp.sum(gram_a * gram_b) / (batch_total * batch_total)
    missing = 1.0 - diagonal
    on_diagonal = jnp.sum(missing * missing - redundancy * diagonal * diagonal)
    loss_value = (
        redundancy * lax.psum(square_sum, "batch") + lax.psum(on_diagonal, "feat")
    ) / feature_total
    ddiag = (2.0 * (diagonal - 1.0)).astype(jnp.bfloat16).astype(jnp.float32)
    rest = ddiag - 2.0 * redundancy * diagonal
    dnorm_a = scale * jnp.dot(
        gram_b.astype(jnp.bfloat16), samples_a, preferred_element_type=jnp.float32
    ) + low_b.astype(jnp.float32) * rest
    dnorm_b = scale * jnp.dot(
        gram_a.astype(jnp.bfloat16), samples_b, preferred_element_type=jnp.float32
    ) + low_a.astype(jnp.float32) * rest
    grad_totals = lax.psum(
        jnp.stack([
            jnp.sum(dnorm_a, axis=0),
            jnp.sum(dnorm_a * normed_a, axis=0),
            jnp.sum(dnorm_b, axis=0),
            jnp.sum(dnorm_b * normed_b, axis=0),
        ]),
        "batch",
    ) / batch_total
    grad_a = (dnorm_a - grad_totals[0] - normed_a * grad_totals[1]) * factor_a
    grad_b = (dnorm_b - grad_totals[2] - normed_b * grad_totals[3]) * factor_b
    return (loss_value, grad_a, grad_b)


def solution(mesh):
    return jax.shard_map(
        local,
        mesh=mesh,
        in_specs=(P("batch", "feat"), P("batch", "feat")),
        out_specs=(P(), P("batch", "feat"), P("batch", "feat")),
        check_vma=False,
    )
```

time: 460 us -> 215 us (0.47)
  waiting for transfers between devices: 304 us -> 138 us
  blocking collectives: 76.9 us -> 30.8 us
  matrix products: 35.8 us -> 10.6 us
  local copies, waits for them, and re-layouts: 8.95 us -> 1.93 us
  starting transfers between devices: 5.07 us -> 0.11 us
    all_gather x3 -> x2, waiting for transfers between devices: 265 us -> 71.8 us  [the longest x1 39.1 us: local(): lax.all_gather(view_b, 'batch', axis=0, tiled=True).astype(jnp.float32)]
    psum x0 -> x1, waiting for transfers between devices: none -> 64.7 us  [local(): gram_a, gram_b = lax.psum((gram_a, gram_b), 'feat')]
    psum x4 -> x2, blocking collectives: 76.9 us -> 30.8 us  [the longest x1 16.7 us: local(): lax.psum(square_sum, 'batch')]
    reduce_scatter x1 -> x0, waiting for transfers between devices: 39.2 us -> none  [local(): lax.psum_scatter(lax.dot_general(column, low_b, (((1,), (1,)), ((), ())),...]
    dot_general x3 -> x4, matrix products: 35.8 us -> 10.6 us  [the longest x1 3.71 us: local(): jnp.dot(gram_a.astype(jnp.bfloat16), samples_b, preferred_element_type=jn...]
    reduce_sum x6 -> x7, other arithmetic: 6.06 us -> 12.9 us  [the longest x2 4.39 us: normalize(): factor = lax.rsqrt(jnp.mean(shifted * shifted, axis=0) + variance_floor)]
    all_to_all x1 -> x0, local copies, waits for them, and re-layouts: 6.39 us -> none  [local(): lax.all_to_all(whole_a, 'batch', split_axis=1, concat_axis=0, tiled=True)]
    all_to_all x1 -> x0, starting transfers between devices: 4.91 us -> none  [local(): lax.all_to_all(whole_a, 'batch', split_axis=1, concat_axis=0, tiled=True)]
  transfers between devices with their start and end apart: 5 -> 3, of which waited for: 4 -> 3; matrix products, arithmetic and copies ran while one was open for 4% -> 2% of each run, Pallas kernels for 0% -> 0%
where the time goes in v1:
time: 215 us
  waiting for transfers between devices  138 us (64%)
  blocking collectives  30.8 us (14%)
  between operations  16.9 us (8%)
  other arithmetic  16.7 us (8%)
  matrix products  10.6 us (5%)
    psum x1, waiting for transfers between devices, local(): gram_a, gram_b = lax.psum((gram_a, gram_b), 'feat')  64.7 us
    all_gather x1, waiting for transfers between devices, local(): lax.all_gather(view_b, 'batch', axis=0, tiled=True).astype(jnp.float32)  39.1 us
    all_gather x1, waiting for transfers between devices, local(): lax.all_gather(view_a, 'batch', axis=0, tiled=True).astype(jnp.float32)  32.7 us
    psum x1, blocking collectives, local(): lax.psum(square_sum, 'batch')  16.7 us
    psum x1, blocking collectives, local(): lax.psum(on_diagonal, 'feat')  14.1 us
    reduce_sum x2, other arithmetic, normalize(): factor = lax.rsqrt(jnp.mean(shifted * shifted, axis=0) + variance_floor)  4.39 us
  transfers between devices with their start and end apart: 3, of which 3 were waited for; matrix products, arithmetic and copies ran while one was open for 2% of the time, Pallas kernels for 0%

profile of v1, /device:TPU:0, one launch (start us, length us, event | category | flops | bytes accessed | tf_op | source)
XLA Modules:
  0.0 214.9 jit_solution(2720417715191200005)
XLA Ops:
  7.2 0.0 all-gather.5.cloned.1.call-start
  7.2 0.7 all-gather.5.cloned.1.call-update
  7.9 0.0 all-gather.3.cloned.1.call-start
  7.9 0.7 all-gather.3.cloned.1.call-update
  8.6 0.0 all-reduce.4.cloned.1.call-start
  8.7 39.1 %all-gather.5.cloned.1.call-done = bf16[1024,1024]{1,0:T(8,128)(2,1)} async-done(((bf16[256,1024]{1,0:T(8,128)(2,1)}), bf16[1024,1024]{1,0:T(8,128)(2,1)}) %all-gather.5.cloned.1.call-update) | async-done | bytes 2097168 | tf_op jit(solution)/shard_map/all_gather | solution.py:17
  47.8 0.0 copy-start
  47.8 2.1 convert_reduce_fusion
  49.9 2.2 %fusion.4 = f32[1024]{0:T(1024)S(1)} fusion(bf16[1024,1024]{1,0:T(8,128)(2,1)} %all-gather.5.cloned.1.call-done, f32[1024]{0:T(1024)S(1)} %broadcast_multiply_fusion.1), kind=kLoop, calls=%fused_computation.8 | loop fusion | flops 4193280 | bytes 2105344 | tf_op jit(solution)/shard_map/reduce_sum | solution.py:21
  52.1 32.7 %all-gather.3.cloned.1.call-done = bf16[1024,1024]{1,0:T(8,128)(2,1)} async-done(((bf16[256,1024]{1,0:T(8,128)(2,1)}), bf16[1024,1024]{1,0:T(8,128)(2,1)}) %all-gather.3.cloned.1.call-update) | async-done | bytes 2097168 | tf_op jit(solution)/shard_map/all_gather | solution.py:16
  84.8 0.0 copy-start.1
  84.8 2.1 convert_reduce_fusion.1
  86.9 2.2 %fusion.5 = f32[1024]{0:T(1024)S(1)} fusion(bf16[1024,1024]{1,0:T(8,128)(2,1)} %all-gather.3.cloned.1.call-done, f32[1024]{0:T(1024)S(1)} %broadcast_multiply_fusion.2), kind=kLoop, calls=%fused_computation.9 | loop fusion | flops 4193280 | bytes 2105344 | tf_op jit(solution)/shard_map/reduce_sum | solution.py:21
  89.1 0.0 copy-done
  89.1 0.0 copy-done.1
  89.1 1.3 multiply_reduce_fusion
  90.4 0.0 copy-start.3
  90.4 0.0 copy-start.2
  90.4 1.9 copy-done.3
  92.4 1.7 fusion.10
  94.1 0.0 copy-done.2
  94.1 1.7 fusion.14
  95.8 0.0 all-reduce.4.cloned.1.call-update
  95.8 0.6 subtract_reduce_fusion
  96.5 64.7 %all-reduce.4.cloned.1.call-done = (f32[256,1024]{1,0:T(8,128)}, f32[256,1024]{1,0:T(8,128)}) async-done(((f32[256,1024]{1,0:T(8,128)}, f32[256,1024]{1,0:T(8,128)}), (f32[256,1024]{1,0:T(8,128)}, f32[256,1024]{1,0:T(8,128)})) %all-reduce.4.cloned.1.call-update) | async-done | bytes 2097168 | tf_op jit(solution)/shard_map/psum | solution.py:40
  161.2 2.4 %multiply_reduce_fusion.3 = f32[]{:T(128)} fusion(f32[256,1024]{1,0:T(8,128)} %get-tuple-element.7, f32[256,1024]{1,0:T(8,128)} %get-tuple-element.8), kind=kLoop, calls=%fused_computation.19 | loop fusion | flops 524287 | bytes 2097156 | tf_op jit(solution)/shard_map/reduce_sum | solution.py:41
  164.2 3.4 %fusion.20 = (f32[1024]{0:T(1024)S(1)}, f32[1024]{0:T(1024)S(1)}, f32[256,1024]{1,0:T(8,128)S(1)}) fusion(f32[1024,1024]{1,0:T(8,128)} %copy-done.2, s32[]{:T(128)S(6)} %select_n.4, f32[1024]{0:T(1024)S(1)} %get-tuple-element.19, f32[1024,1024]{1,0:T(8,128)} %copy-done.3, f32[1024]{0:T(1024)S(1)} %add_rsqrt_fusion.1, ...), kind=kOutput, calls=%fused_computation.39 | convolution fusion | flops 543160320 | bytes 5787652 | tf_op jit(solution)/shard_map/dot_general | solution.py:49
  167.6 3.7 %fusion.21 = (f32[1024]{0:T(1024)S(1)}, f32[1024]{0:T(1024)S(1)}, f32[256,1024]{1,0:T(8,128)}) fusion(f32[1024,1024]{1,0:T(8,128)} %copy-done.3, s32[]{:T(128)S(6)} %select_n.4, f32[1024]{0:T(1024)S(1)} %get-tuple-element.19, f32[1024,1024]{1,0:T(8,128)} %copy-done.2, f32[1024]{0:T(1024)S(1)} %add_rsqrt_fusion, f32[1024]{0:T(1024)S(1)} %broadcast_multiply_fusion.1, ...), kind=kOutput, calls=%fused_computation.40 | convolution fusion | flops 543160320 | bytes 5787652 | tf_op jit(solution)/shard_map/dot_general | solution.py:52
  171.3 14.1 %psum.38 = f32[]{:T(128)} all-reduce(f32[]{:T(128)} %get-tuple-element.18), channel_id=1, replica_groups=mesh['batch'=4,'feat'=8] {'feat'}, use_global_device_ids=true, to_apply=%region_10.0 | all-reduce | flops 1 | bytes 8 | tf_op jit(solution)/shard_map/psum | solution.py:45
  185.4 16.7 %all-reduce.1 = (f32[]{:T(128)}, f32[4,1024]{1,0:T(4,128)S(1)}) all-reduce(f32[]{:T(128)S(6)} %div.31, f32[4,1024]{1,0:T(4,128)S(1)} %pad_maximum_fusion), channel_id=1, replica_groups=mesh['batch'=4,'feat'=8] {'batch'}, use_global_device_ids=true, to_apply=%region_7.0 | all-reduce | flops 4097 | bytes 32776 | tf_op jit(solution)/shard_map/psum | solution.py:45
  203.4 3.8 %subtract_multiply_fusion = (f32[256,1024]{1,0:T(8,128)}, f32[256,1024]{1,0:T(8,128)}) fusion(f32[256,1024]{1,0:T(8,128)} %get-tuple-element.20, f32[1024,1024]{1,0:T(8,128)} %copy-done.3, s32[]{:T(128)S(6)} %select_n.4, f32[1024]{0:T(1024)S(1)} %add_rsqrt_fusion, f32[1024]{0:T(1024)S(1)} %bitcast.9, f32[1024]{0:T(1024)S(1)} %bitcast.8, ...), kind=kLoop, calls=%fused_computation.15 | loop fusion | flops 2097152 | bytes 6316036 | tf_op jit(solution)/shard_map/mul | solution.py:65
  (7 shorter events, 0.1 us)
Async XLA Ops:
  7.2 40.6 %all-gather.5.cloned.1.call-start = ((), (), s32[]{:S(2)}) async-start(), calls=%async_computation.1 | async-start | bytes 2621440 | tf_op jit(solution)/shard_map/all_gather | solution.py:17
  7.9 76.9 %all-gather.3.cloned.1.call-start = ((), (), s32[]{:S(2)}) async-start(), calls=%async_computation | async-start | bytes 2621440 | tf_op jit(solution)/shard_map/all_gather | solution.py:16
  8.6 152.5 %all-reduce.4.cloned.1.call-start = ((), (), s32[]{:S(2)}) async-start(), calls=%async_computation.2 | async-start | bytes 4194304 | tf_op jit(solution)/shard_map/psum | solution.py:40
  47.8 41.4 %copy-start = (bf16[1024,1024]{1,0:T(8,128)(2,1)S(1)}, bf16[1024,1024]{1,0:T(8,128)(2,1)}, u32[]{:S(2)}) copy-start(bf16[1024,1024]{1,0:T(8,128)(2,1)} %all-gather.5.cloned.1.call-done) | copy-start | bytes 6291460
  84.8 4.3 %copy-start.1 = (bf16[1024,1024]{1,0:T(8,128)(2,1)S(1)}, bf16[1024,1024]{1,0:T(8,128)(2,1)}, u32[]{:S(2)}) copy-start(bf16[1024,1024]{1,0:T(8,128)(2,1)} %all-gather.3.cloned.1.call-done) | copy-start | bytes 6291460
  90.4 1.9 copy-start.3
  90.4 3.7 %copy-start.2 = (f32[1024,1024]{1,0:T(8,128)}, f32[1024,1024]{1,0:T(8,128)S(1)}, u32[]{:S(2)}) copy-start(f32[1024,1024]{1,0:T(8,128)S(1)} %get-tuple-element.12) | copy-start | bytes 12582916
Sparse Core Ops, SparseCore 0:
  9.8 37.8 all-gather.4
  49.6 35.1 all-gather.2
  96.0 65.1 all-reduce.3

commit v2 on v1

--- a/solution.py
+++ b/solution.py
@@ -1,13 +1,20 @@
+import functools
+
 import jax
 import jax.numpy as jnp
 from jax import lax
+from jax.experimental import pallas as pl
+from jax.experimental.pallas import tpu as pltpu
 from jax.sharding import PartitionSpec as P
+
+MESH = pl.DeviceIdType.MESH
+ROWS_T = (((1,), (1,)), ((), ()))
 
 variance_floor = 0.25
 redundancy = 0.0051
 
 
-def local(view_a, view_b):
+def plain(view_a, view_b):
     rows_dev, cols_dev = view_a.shape
     groups = lax.axis_size("batch")
     batch_total = rows_dev * groups
@@ -66,9 +73,412 @@
     return (loss_value, grad_a, grad_b)
 
 
+def fold(values):
+    rows, cols = values.shape
+    return jnp.sum(values.reshape(rows // 8, 8, cols), axis=0)
+
+
+def column_sums(rows, cols, count, term, step=16):
+    zero = jnp.zeros((8, cols), jnp.float32)
+
+    def body(i, carry):
+        pieces = term(pl.ds(pl.multiple_of(i * step, step), step))
+        return tuple(c + fold(p) for c, p in zip(carry, pieces))
+
+    sums = lax.fori_loop(0, rows // step, body, (zero,) * count)
+    return tuple(jnp.sum(s, axis=0, keepdims=True) for s in sums)
+
+
+def kernel(
+    feats, view_a, view_b, loss_ref, grad_a, grad_b,
+    raw, low, part, pair_in, sum0, in0, sum1, in1, gram0, gram, rest0,
+    stats, finals, losses,
+    g_send, g_recv, s_send, s_recv, p_send, p_recv, z_send, z_recv,
+    w_send, w_recv, q_send, q_recv, f_send, f_recv, l_send, l_recv,
+):
+    views, grads = (view_a, view_b), (grad_a, grad_b)
+    rows, cols = view_a.shape
+    half = rows // 2
+    groups = 4
+    depth = feats // 2
+    share = half // depth
+    samples = rows * groups
+    features = cols * feats
+    devices = groups * feats
+    group, owner = lax.axis_index("batch"), lax.axis_index("feat")
+    gy, gx = group // 2, group % 2
+    peers = (gy * 2 + 1 - gx, (1 - gy) * 2 + gx, (1 - gy) * 2 + 1 - gx)
+    z, core = owner // 2, owner % 2
+    partner = z * 2 + 1 - core
+    mine = pl.ds(pl.multiple_of(core * half, half), half)
+    theirs = pl.ds(pl.multiple_of((1 - core) * half, half), half)
+    me = group * feats + owner
+    sent = []
+
+    def send(src, dst, ssem, rsem, device):
+        copy = pltpu.make_async_remote_copy(
+            src_ref=src, dst_ref=dst, send_sem=ssem, recv_sem=rsem,
+            device_id=device, device_id_type=MESH,
+        )
+        copy.start()
+        sent.append(copy)
+        return copy
+
+    barrier = pltpu.get_barrier_semaphore()
+
+    @pl.loop(1, devices)
+    def _(k):
+        other = (me + k) % devices
+        pl.semaphore_signal(
+            barrier, inc=1,
+            device_id={"batch": other // feats, "feat": other % feats},
+            device_id_type=MESH,
+        )
+
+    pl.semaphore_wait(barrier, devices - 1)
+
+    lower, upper = pl.ds(0, half), pl.ds(half, half)
+    moves = {}
+
+    def own(v, link, part_of):
+        index = link * 2 + part_of
+        span = (lower, upper)[part_of]
+        moves[v, link, part_of] = send(
+            views[v].at[span], raw.at[v, link, span],
+            g_send.at[v, index], g_recv.at[v, index], {"batch": peers[link]},
+        )
+
+    def forward(v):
+        for link, part_of in ((0, 0), (1, 1)):
+            moves[v, link, part_of].wait_recv()
+            span = (lower, upper)[part_of]
+            moves[v, 2, part_of] = send(
+                raw.at[v, link, span], raw.at[v, 2, span],
+                g_send.at[v, 4 + part_of], g_recv.at[v, 4 + part_of],
+                {"batch": peers[1 - link]},
+            )
+
+    own(0, 0, 0)
+    own(0, 1, 1)
+
+    means = column_sums(
+        rows, cols, 2,
+        lambda r: tuple(x[r].astype(jnp.float32) for x in views),
+    )
+    means = tuple(m / rows for m in means)
+
+    def squares(r):
+        shifted = tuple(x[r].astype(jnp.float32) - m for x, m in zip(views, means))
+        return tuple(s * s for s in shifted)
+
+    spreads = column_sums(rows, cols, 2, squares)
+    stats[0, 0:1] = means[0]
+    stats[0, 1:2] = means[1]
+    stats[0, 2:3] = spreads[0]
+    stats[0, 3:4] = spreads[1]
+    stat_moves = [
+        send(stats.at[0], stats.at[k + 1], s_send.at[k], s_recv.at[k], {"batch": peers[k]})
+        for k in range(3)
+    ]
+    own(0, 0, 1)
+    own(0, 1, 0)
+    for move in stat_moves:
+        move.wait_recv()
+
+    def merged(row):
+        first = [stats[k, row : row + 1] for k in range(4)]
+        return first, (first[0] + first[1]) + (first[2] + first[3])
+
+    centers, factors = [], []
+    for v in range(2):
+        each, total = merged(v)
+        center = total / groups
+        gaps = [(e - center) * (e - center) for e in each]
+        gap = (gaps[0] + gaps[1]) + (gaps[2] + gaps[3])
+        variance = (merged(2 + v)[1] + rows * gap) / samples
+        centers.append(center)
+        factors.append(lax.rsqrt(variance + variance_floor))
+
+    def normalize(v, slot):
+        source = views[v] if slot == 0 else raw.at[v, slot - 1]
+
+        @pl.loop(0, rows // 16)
+        def _(i):
+            r = pl.ds(pl.multiple_of(i * 16, 16), 16)
+            values = source[r].astype(jnp.float32)
+            low[v, slot, r] = ((values - centers[v]) * factors[v]).astype(jnp.bfloat16)
+
+    ring = {}
+
+    def buffers(v, slot):
+        p = v * 4 + slot
+        if slot == 0:
+            return p, sum0.at[v], in0.at[v], gram0.at[v]
+        return p, sum1.at[v, slot - 1], in1.at[v, slot - 1], gram.at[v, slot]
+
+    def product(v, slot):
+        p = v * 4 + slot
+        part[p] = lax.dot_general(
+            low[v, 0], low[v, slot], ROWS_T, preferred_element_type=jnp.float32
+        )
+        ring["pair", p] = send(
+            part.at[p, theirs], pair_in.at[p], p_send.at[p], p_recv.at[p], {"feat": partner}
+        )
+
+    def scatter(v, slot):
+        p, total, arrivals, _ = buffers(v, slot)
+        ring["pair", p].wait_recv()
+        total[...] = (part[p, mine] + pair_in[p]).astype(total.dtype)
+        for k in range(1, depth):
+            target = (z + k) % depth
+            ring["sum", p, k] = send(
+                total.at[pl.ds(pl.multiple_of(target * share, share), share)],
+                arrivals.at[k - 1], z_send.at[p, k - 1], z_recv.at[p, k - 1],
+                {"feat": target * 2 + core},
+            )
+
+    def collect(v, slot):
+        p, total, arrivals, result = buffers(v, slot)
+        value = total[pl.ds(pl.multiple_of(z * share, share), share)].astype(jnp.float32)
+        for k in range(1, depth):
+            ring["sum", p, k].wait_recv()
+            value = value + arrivals[k - 1].astype(jnp.float32)
+        span = pl.ds(pl.multiple_of(core * half + z * share, share), share)
+        result[span] = value.astype(result.dtype)
+        for k in range(1, depth):
+            ring["all", p, k] = send(
+                result.at[span], result.at[span], w_send.at[p, k - 1], w_recv.at[p, k - 1],
+                {"feat": (z + k) % depth * 2 + core},
+            )
+
+    def swap(v, slot):
+        p, _, _, result = buffers(v, slot)
+        for k in range(1, depth):
+            ring["all", p, k].wait_recv()
+        ring["swap", p] = send(
+            result.at[mine], result.at[mine], q_send.at[p], q_recv.at[p], {"feat": partner}
+        )
+
+    def finish(v, slot):
+        ring["swap", v * 4 + slot].wait_recv()
+        if slot == 0:
+            high = gram0[v].astype(jnp.bfloat16)
+            gram[v, 0] = high
+            rest0[v] = (gram0[v] - high.astype(jnp.float32)).astype(jnp.bfloat16)
+
+    forward(0)
+    for link, part_of in ((0, 0), (1, 1), (0, 1), (1, 0)):
+        own(1, link, part_of)
+    normalize(0, 0)
+    product(0, 0)
+    normalize(1, 0)
+    product(1, 0)
+    scatter(0, 0)
+    scatter(1, 0)
+    moves[0, 0, 1].wait_recv()
+    normalize(0, 1)
+    product(0, 1)
+    moves[0, 1, 0].wait_recv()
+    normalize(0, 2)
+    product(0, 2)
+    collect(0, 0)
+    collect(1, 0)
+    scatter(0, 1)
+    scatter(0, 2)
+    swap(0, 0)
+    swap(1, 0)
+    moves[0, 2, 0].wait_recv()
+    moves[0, 2, 1].wait_recv()
+    normalize(0, 3)
+    product(0, 3)
+    collect(0, 1)
+    collect(0, 2)
+    scatter(0, 3)
+    finish(0, 0)
+    finish(1, 0)
+    swap(0, 1)
+    swap(0, 2)
+    forward(1)
+    collect(0, 3)
+    finish(0, 1)
+    finish(0, 2)
+    moves[1, 0, 1].wait_recv()
+    normalize(1, 1)
+    product(1, 1)
+    moves[1, 1, 0].wait_recv()
+    normalize(1, 2)
+    product(1, 2)
+    swap(0, 3)
+    scatter(1, 1)
+    scatter(1, 2)
+    collect(1, 1)
+    collect(1, 2)
+    finish(0, 3)
+    swap(1, 1)
+    swap(1, 2)
+    moves[1, 2, 0].wait_recv()
+    moves[1, 2, 1].wait_recv()
+    normalize(1, 3)
+    product(1, 3)
+    scatter(1, 3)
+
+    def term(slot):
+        return lambda r: (
+            low[0, slot, r].astype(jnp.float32) * low[1, slot, r].astype(jnp.float32),
+        )
+
+    diagonal = sum(column_sums(rows, cols, 1, term(slot))[0] for slot in range(4)) / samples
+    missing = 1.0 - diagonal
+    on_diagonal = jnp.sum(missing * missing - redundancy * diagonal * diagonal)
+    ddiag = (2.0 * (diagonal - 1.0)).astype(jnp.bfloat16).astype(jnp.float32)
+    rest = ddiag - 2.0 * redundancy * diagonal
+    scale = 2.0 * redundancy / samples
+    collect(1, 3)
+
+    width = min(256, cols)
+
+    def spread(v, slots, add):
+        other = 1 - v
+
+        @pl.loop(0, cols // width)
+        def _(i):
+            c = pl.ds(pl.multiple_of(i * width, width), width)
+            if add:
+                total = grads[other][:, c]
+            else:
+                total = jnp.dot(rest0[v], low[other, 0, :, c], preferred_element_type=jnp.float32)
+            for slot in slots:
+                total = total + jnp.dot(
+                    gram[v, slot], low[other, slot, :, c], preferred_element_type=jnp.float32
+                )
+            grads[other][:, c] = total
+
+    final_moves = {}
+
+    def reduce_final(v):
+        def body(r):
+            dnorm = scale * grads[v][r] + low[1 - v, 0, r].astype(jnp.float32) * rest
+            normed = (views[v][r].astype(jnp.float32) - centers[v]) * factors[v]
+            grads[v][r] = dnorm
+            return dnorm, dnorm * normed
+
+        first, second = column_sums(rows, cols, 2, body)
+        finals[v, 0, 0:1] = first
+        finals[v, 0, 1:2] = second
+        for k in range(3):
+            final_moves[v, k] = send(
+                finals.at[v, 0], finals.at[v, k + 1], f_send.at[v, k], f_recv.at[v, k],
+                {"batch": peers[k]},
+            )
+
+    def write_final(v):
+        for k in range(3):
+            final_moves[v, k].wait_recv()
+        first, second = (
+            ((finals[v, 0, i : i + 1] + finals[v, 1, i : i + 1])
+             + (finals[v, 2, i : i + 1] + finals[v, 3, i : i + 1])) / samples
+            for i in range(2)
+        )
+
+        @pl.loop(0, rows // 16)
+        def _(i):
+            r = pl.ds(pl.multiple_of(i * 16, 16), 16)
+            normed = (views[v][r].astype(jnp.float32) - centers[v]) * factors[v]
+            grads[v][r] = (grads[v][r] - first - normed * second) * factors[v]
+
+    finish(1, 1)
+    finish(1, 2)
+    spread(0, range(4), False)
+    swap(1, 3)
+    reduce_final(1)
+    spread(1, range(3), False)
+    finish(1, 3)
+    spread(1, (3,), True)
+    reduce_final(0)
+
+    def gram_term(slot):
+        def body(r):
+            if slot == 0:
+                return (gram0[0, r] * gram0[1, r],)
+            return (gram[0, slot, r].astype(jnp.float32) * gram[1, slot, r].astype(jnp.float32),)
+
+        return body
+
+    square = sum(column_sums(rows, rows, 1, gram_term(slot))[0] for slot in range(4))
+    square_sum = jnp.sum(square) / (samples * samples)
+    share_of_loss = redundancy * square_sum / feats + on_diagonal / groups
+    losses[me] = jnp.full((8, 128), share_of_loss, jnp.float32)
+
+    def loss_copy(k):
+        other = (me + k) % devices
+        return pltpu.make_async_remote_copy(
+            src_ref=losses.at[me], dst_ref=losses.at[me], send_sem=l_send, recv_sem=l_recv,
+            device_id={"batch": other // feats, "feat": other % feats}, device_id_type=MESH,
+        )
+
+    @pl.loop(1, devices)
+    def _(k):
+        loss_copy(k).start()
+
+    write_final(1)
+    write_final(0)
+    rest_of = losses.at[pl.ds(0, devices - 1)]
+    pltpu.make_async_copy(rest_of, rest_of, l_recv).wait()
+    loss_ref[...] = jnp.sum(losses[...], axis=0) / features
+    pltpu.make_async_copy(rest_of, rest_of, l_send).wait()
+    for copy in sent:
+        copy.wait_send()
+
+
+def local(feats, view_a, view_b):
+    rows, cols = view_a.shape
+    half, depth = rows // 2, feats // 2
+    share = half // depth
+    f32, bf16 = jnp.float32, jnp.bfloat16
+    dma = pltpu.SemaphoreType.DMA
+    vmem = pl.BlockSpec(memory_space=pltpu.VMEM)
+    loss, grad_a, grad_b = pl.pallas_call(
+        functools.partial(kernel, feats),
+        out_shape=(
+            jax.ShapeDtypeStruct((8, 128), f32),
+            jax.ShapeDtypeStruct((rows, cols), f32),
+            jax.ShapeDtypeStruct((rows, cols), f32),
+        ),
+        in_specs=[vmem, vmem],
+        out_specs=(vmem, vmem, vmem),
+        scratch_shapes=[
+            pltpu.VMEM((2, 3, rows, cols), bf16),
+            pltpu.VMEM((2, 4, rows, cols), bf16),
+            pltpu.VMEM((8, rows, rows), f32),
+            pltpu.VMEM((8, half, rows), f32),
+            pltpu.VMEM((2, half, rows), f32),
+            pltpu.VMEM((2, depth - 1, share, rows), f32),
+            pltpu.VMEM((2, 3, half, rows), bf16),
+            pltpu.VMEM((2, 3, depth - 1, share, rows), bf16),
+            pltpu.VMEM((2, rows, rows), f32),
+            pltpu.VMEM((2, 4, rows, rows), bf16),
+            pltpu.VMEM((2, rows, rows), bf16),
+            pltpu.VMEM((4, 4, cols), f32),
+            pltpu.VMEM((2, 4, 2, cols), f32),
+            pltpu.VMEM((4 * feats, 8, 128), f32),
+            dma((2, 6)), dma((2, 6)), dma((3,)), dma((3,)),
+            dma((8,)), dma((8,)), dma((8, depth - 1)), dma((8, depth - 1)),
+            dma((8, depth - 1)), dma((8, depth - 1)), dma((8,)), dma((8,)),
+            dma((2, 3)), dma((2, 3)), dma, dma,
+        ],
+        compiler_params=pltpu.CompilerParams(
+            collective_id=0, has_side_effects=True, vmem_limit_bytes=56 * 1024 * 1024
+        ),
+        name="twins",
+    )(view_a, view_b)
+    return loss[0, 0], grad_a, grad_b
+
+
 def solution(mesh):
+    feats = mesh.shape["feat"]
+    body = functools.partial(local, feats) if mesh.shape["batch"] == 4 else plain
     return jax.shard_map(
-        local,
+        body,
         mesh=mesh,
         in_specs=(P("batch", "feat"), P("batch", "feat")),
         out_specs=(P(), P("batch", "feat"), P("batch", "feat")),

time: 215 us -> 78.1 us (0.36)
  waiting for transfers between devices: 138 us -> 0 us
  Pallas kernels: 0 us -> 72.7 us
  blocking collectives: 30.8 us -> 0 us
  other arithmetic: 16.7 us -> 0 us
  between operations: 16.9 us -> 0.64 us
  matrix products: 10.6 us -> 0 us
  local copies, waits for them, and re-layouts: 1.93 us -> 4.56 us
    pallas_call x0 -> x1, Pallas kernels: none -> 72.7 us  [local(): pl.pallas_call(functools.partial(kernel, feats), out_shape=(jax.ShapeDtyp...]
    all_gather x2 -> x0, waiting for transfers between devices: 71.8 us -> none  [the longest x1 39.1 us: local(): lax.all_gather(view_b, 'batch', axis=0, tiled=True).astype(jnp.float32)]
    psum x1 -> x0, waiting for transfers between devices: 64.7 us -> none  [local(): gram_a, gram_b = lax.psum((gram_a, gram_b), 'feat')]
    psum x2 -> x0, blocking collectives: 30.8 us -> none  [the longest x1 16.7 us: local(): lax.psum(square_sum, 'batch')]
    reduce_sum x7 -> x0, other arithmetic: 12.9 us -> none  [the longest x2 4.39 us: normalize(): factor = lax.rsqrt(jnp.mean(shifted * shifted, axis=0) + variance_floor)]
    dot_general x4 -> x0, matrix products: 10.6 us -> none  [the longest x1 3.71 us: local(): jnp.dot(gram_a.astype(jnp.bfloat16), samples_b, preferred_element_type=jn...]
    mul x1 -> x0, other arithmetic: 3.76 us -> none  [local(): grad_b = (dnorm_b - grad_totals[2] - normed_b * grad_totals[3]) * factor_b]
  transfers between devices with their start and end apart: 3 -> 0, of which waited for: 3 -> 0; matrix products, arithmetic and copies ran while one was open for 2% -> 0% of each run, Pallas kernels for 0% -> 0%
where the time goes in v2:
time: 78.1 us; the launch traced here: 77.9 us
  Pallas kernels  72.7 us (93%)
  local copies, waits for them, and re-layouts  4.56 us (6%)
    pallas_call x1, Pallas kernels, local(): pl.pallas_call(functools.partial(kernel, feats), out_shape=(jax.ShapeDtyp...  72.7 us
    unnamed x4, local copies, waits for them, and re-layouts  3.37 us

profile of v2, /device:TPU:0, one launch (start us, length us, event | category | flops | bytes accessed | tf_op | source)
XLA Modules:
  0.0 77.9 jit_solution(16838255642787301273)
XLA Ops:
  0.6 72.7 %twins.1 = (f32[8,128]{1,0:T(8,128)}, f32[256,1024]{1,0:T(8,128)}, f32[256,1024]{1,0:T(8,128)}) custom-call(bf16[256,1024]{1,0:T(8,128)(2,1)} %view_a.1, bf16[256,1024]{1,0:T(8,128)(2,1)} %view_b.1), custom_call_target="tpu_custom_call" | custom-call | tf_op jit(solution)/shard_map/twins/pallas_call | solution.py:440
  73.3 1.2 %slice.3 = f32[1,1]{1,0:T(1,128)} slice(f32[8,128]{1,0:T(8,128)} %get-tuple-element.6), slice={[0:1], [0:1]} | slice | bytes 8 | tf_op jit(solution)/shard_map/slice | solution.py:474
  74.5 0.0 copy-start
  74.5 2.4 %copy.7 = f32[256,1024]{1,0:T(8,128)} copy(f32[256,1024]{1,0:T(8,128)} %get-tuple-element.13) | data formatting | bytes 2097152
  76.9 0.0 copy-done
  76.9 1.0 %copy.8 = f32[256,1024]{1,0:T(8,128)} copy(f32[256,1024]{1,0:T(8,128)S(1)} %copy-done) | data formatting | bytes 2097152
Async XLA Ops:
  74.5 2.4 %copy-start = (f32[256,1024]{1,0:T(8,128)S(1)}, f32[256,1024]{1,0:T(8,128)}, u32[]{:S(2)}) copy-start(f32[256,1024]{1,0:T(8,128)} %get-tuple-element.14) | copy-start | bytes 3145732

commit v3 on v2

--- a/solution.py
+++ b/solution.py
@@ -90,7 +90,7 @@
 
 
 def kernel(
-    feats, view_a, view_b, loss_ref, grad_a, grad_b,
+    feats, view_a, view_b, table, grad_a, grad_b,
     raw, low, part, pair_in, sum0, in0, sum1, in1, gram0, gram, rest0,
     stats, finals, losses,
     g_send, g_recv, s_send, s_recv, p_send, p_recv, z_send, z_recv,
@@ -104,7 +104,6 @@
     share = half // depth
     samples = rows * groups
     features = cols * feats
-    devices = groups * feats
     group, owner = lax.axis_index("batch"), lax.axis_index("feat")
     gy, gx = group // 2, group % 2
     peers = (gy * 2 + 1 - gx, (1 - gy) * 2 + gx, (1 - gy) * 2 + 1 - gx)
@@ -112,7 +111,6 @@
     partner = z * 2 + 1 - core
     mine = pl.ds(pl.multiple_of(core * half, half), half)
     theirs = pl.ds(pl.multiple_of((1 - core) * half, half), half)
-    me = group * feats + owner
     sent = []
 
     def send(src, dst, ssem, rsem, device):
@@ -126,16 +124,16 @@
 
     barrier = pltpu.get_barrier_semaphore()
 
-    @pl.loop(1, devices)
+    for peer in peers:
+        pl.semaphore_signal(barrier, inc=1, device_id={"batch": peer}, device_id_type=MESH)
+
+    @pl.loop(1, feats)
     def _(k):
-        other = (me + k) % devices
         pl.semaphore_signal(
-            barrier, inc=1,
-            device_id={"batch": other // feats, "feat": other % feats},
-            device_id_type=MESH,
-        )
-
-    pl.semaphore_wait(barrier, devices - 1)
+            barrier, inc=1, device_id={"feat": (owner + k) % feats}, device_id_type=MESH
+        )
+
+    pl.semaphore_wait(barrier, len(peers) + feats - 1)
 
     lower, upper = pl.ds(0, half), pl.ds(half, half)
     moves = {}
@@ -199,12 +197,13 @@
         centers.append(center)
         factors.append(lax.rsqrt(variance + variance_floor))
 
-    def normalize(v, slot):
+    def normalize(v, slot, part_of=None):
         source = views[v] if slot == 0 else raw.at[v, slot - 1]
-
-        @pl.loop(0, rows // 16)
+        count, base = (rows, 0) if part_of is None else (half, part_of * half)
+
+        @pl.loop(0, count // 16)
         def _(i):
-            r = pl.ds(pl.multiple_of(i * 16, 16), 16)
+            r = pl.ds(pl.multiple_of(base + i * 16, 16), 16)
             values = source[r].astype(jnp.float32)
             low[v, slot, r] = ((values - centers[v]) * factors[v]).astype(jnp.bfloat16)
 
@@ -266,74 +265,13 @@
             gram[v, 0] = high
             rest0[v] = (gram0[v] - high.astype(jnp.float32)).astype(jnp.bfloat16)
 
-    forward(0)
-    for link, part_of in ((0, 0), (1, 1), (0, 1), (1, 0)):
-        own(1, link, part_of)
-    normalize(0, 0)
-    product(0, 0)
-    normalize(1, 0)
-    product(1, 0)
-    scatter(0, 0)
-    scatter(1, 0)
-    moves[0, 0, 1].wait_recv()
-    normalize(0, 1)
-    product(0, 1)
-    moves[0, 1, 0].wait_recv()
-    normalize(0, 2)
-    product(0, 2)
-    collect(0, 0)
-    collect(1, 0)
-    scatter(0, 1)
-    scatter(0, 2)
-    swap(0, 0)
-    swap(1, 0)
-    moves[0, 2, 0].wait_recv()
-    moves[0, 2, 1].wait_recv()
-    normalize(0, 3)
-    product(0, 3)
-    collect(0, 1)
-    collect(0, 2)
-    scatter(0, 3)
-    finish(0, 0)
-    finish(1, 0)
-    swap(0, 1)
-    swap(0, 2)
-    forward(1)
-    collect(0, 3)
-    finish(0, 1)
-    finish(0, 2)
-    moves[1, 0, 1].wait_recv()
-    normalize(1, 1)
-    product(1, 1)
-    moves[1, 1, 0].wait_recv()
-    normalize(1, 2)
-    product(1, 2)
-    swap(0, 3)
-    scatter(1, 1)
-    scatter(1, 2)
-    collect(1, 1)
-    collect(1, 2)
-    finish(0, 3)
-    swap(1, 1)
-    swap(1, 2)
-    moves[1, 2, 0].wait_recv()
-    moves[1, 2, 1].wait_recv()
-    normalize(1, 3)
-    product(1, 3)
-    scatter(1, 3)
-
     def term(slot):
         return lambda r: (
             low[0, slot, r].astype(jnp.float32) * low[1, slot, r].astype(jnp.float32),
         )
 
-    diagonal = sum(column_sums(rows, cols, 1, term(slot))[0] for slot in range(4)) / samples
-    missing = 1.0 - diagonal
-    on_diagonal = jnp.sum(missing * missing - redundancy * diagonal * diagonal)
-    ddiag = (2.0 * (diagonal - 1.0)).astype(jnp.bfloat16).astype(jnp.float32)
-    rest = ddiag - 2.0 * redundancy * diagonal
-    scale = 2.0 * redundancy / samples
-    collect(1, 3)
+    def diagonal_sum(slot):
+        return column_sums(rows, cols, 1, term(slot))[0]
 
     width = min(256, cols)
 
@@ -353,6 +291,91 @@
                 )
             grads[other][:, c] = total
 
+    def gram_product(slot):
+        def body(r):
+            if slot == 0:
+                return (gram0[0, r] * gram0[1, r],)
+            return (gram[0, slot, r].astype(jnp.float32) * gram[1, slot, r].astype(jnp.float32),)
+
+        return column_sums(rows, rows, 1, body)[0]
+
+    forward(0)
+    for link, part_of in ((0, 0), (1, 1), (0, 1), (1, 0)):
+        own(1, link, part_of)
+    normalize(0, 0)
+    product(0, 0)
+    normalize(1, 0)
+    product(1, 0)
+    normalize(0, 1, 0)
+    normalize(0, 2, 1)
+    scatter(0, 0)
+    scatter(1, 0)
+    moves[0, 0, 1].wait_recv()
+    normalize(0, 1, 1)
+    product(0, 1)
+    moves[0, 1, 0].wait_recv()
+    normalize(0, 2, 0)
+    product(0, 2)
+    collect(0, 0)
+    collect(1, 0)
+    scatter(0, 1)
+    scatter(0, 2)
+    moves[0, 2, 0].wait_recv()
+    moves[0, 2, 1].wait_recv()
+    normalize(0, 3)
+    product(0, 3)
+    swap(0, 0)
+    swap(1, 0)
+    collect(0, 1)
+    collect(0, 2)
+    scatter(0, 3)
+    finish(0, 0)
+    finish(1, 0)
+    forward(1)
+    normalize(1, 1, 0)
+    normalize(1, 2, 1)
+    swap(0, 1)
+    swap(0, 2)
+    collect(0, 3)
+    diagonal = diagonal_sum(0)
+    square = gram_product(0)
+    finish(0, 1)
+    finish(0, 2)
+    moves[1, 0, 1].wait_recv()
+    normalize(1, 1, 1)
+    product(1, 1)
+    moves[1, 1, 0].wait_recv()
+    normalize(1, 2, 0)
+    product(1, 2)
+    swap(0, 3)
+    scatter(1, 1)
+    scatter(1, 2)
+    diagonal = diagonal + diagonal_sum(1) + diagonal_sum(2)
+    finish(0, 3)
+    spread(0, range(3), False)
+    moves[1, 2, 0].wait_recv()
+    moves[1, 2, 1].wait_recv()
+    normalize(1, 3)
+    product(1, 3)
+    collect(1, 1)
+    collect(1, 2)
+    diagonal = (diagonal + diagonal_sum(3)) / samples
+    missing = 1.0 - diagonal
+    on_diagonal = jnp.sum(missing * missing - redundancy * diagonal * diagonal)
+    scatter(1, 3)
+    losses[owner] = jnp.full((8, 128), on_diagonal, jnp.float32)
+
+    @pl.loop(1, feats)
+    def _(k):
+        pltpu.make_async_remote_copy(
+            src_ref=losses.at[owner], dst_ref=losses.at[owner],
+            send_sem=l_send, recv_sem=l_recv,
+            device_id={"feat": (owner + k) % feats}, device_id_type=MESH,
+        ).start()
+
+    ddiag = (2.0 * (diagonal - 1.0)).astype(jnp.bfloat16).astype(jnp.float32)
+    rest = ddiag - 2.0 * redundancy * diagonal
+    scale = 2.0 * redundancy / samples
     final_moves = {}
 
     def reduce_final(v):
@@ -365,67 +388,54 @@
         first, second = column_sums(rows, cols, 2, body)
         finals[v, 0, 0:1] = first
         finals[v, 0, 1:2] = second
+
+    def exchange_final(v):
         for k in range(3):
             final_moves[v, k] = send(
                 finals.at[v, 0], finals.at[v, k + 1], f_send.at[v, k], f_recv.at[v, k],
                 {"batch": peers[k]},
             )
 
-    def write_final(v):
+    def merge_final(v, count):
         for k in range(3):
             final_moves[v, k].wait_recv()
-        first, second = (
-            ((finals[v, 0, i : i + 1] + finals[v, 1, i : i + 1])
-             + (finals[v, 2, i : i + 1] + finals[v, 3, i : i + 1])) / samples
-            for i in range(2)
-        )
-
-        @pl.loop(0, rows // 16)
-        def _(i):
-            r = pl.ds(pl.multiple_of(i * 16, 16), 16)
-            normed = (views[v][r].astype(jnp.float32) - centers[v]) * factors[v]
-            grads[v][r] = (grads[v][r] - first - normed * second) * factors[v]
-
+        return tuple(
+            (finals[v, 0, i : i + 1] + finals[v, 1, i : i + 1])
+            + (finals[v, 2, i : i + 1] + finals[v, 3, i : i + 1])
+            for i in range(count)
+        )
+
+    spread(0, (3,), True)
+    collect(1, 3)
+    swap(1, 1)
+    swap(1, 2)
+    reduce_final(1)
+    exchange_final(1)
     finish(1, 1)
     finish(1, 2)
-    spread(0, range(4), False)
+    spread(1, range(3), False)
     swap(1, 3)
-    reduce_final(1)
-    spread(1, range(3), False)
+    square = square + gram_product(1) + gram_product(2)
+    rest_of = losses.at[pl.ds(0, feats - 1)]
+    pltpu.make_async_copy(rest_of, rest_of, l_recv).wait()
+    on_diagonal_all = jnp.sum(losses[...], axis=0)[0:1, 0:1]
     finish(1, 3)
     spread(1, (3,), True)
     reduce_final(0)
-
-    def gram_term(slot):
-        def body(r):
-            if slot == 0:
-                return (gram0[0, r] * gram0[1, r],)
-            return (gram[0, slot, r].astype(jnp.float32) * gram[1, slot, r].astype(jnp.float32),)
-
-        return body
-
-    square = sum(column_sums(rows, rows, 1, gram_term(slot))[0] for slot in range(4))
-    square_sum = jnp.sum(square) / (samples * samples)
-    share_of_loss = redundancy * square_sum / feats + on_diagonal / groups
-    losses[me] = jnp.full((8, 128), share_of_loss, jnp.float32)
-
-    def loss_copy(k):
-        other = (me + k) % devices
-        return pltpu.make_async_remote_copy(
-            src_ref=losses.at[me], dst_ref=losses.at[me], send_sem=l_send, recv_sem=l_recv,
-            device_id={"batch": other // feats, "feat": other % feats}, device_id_type=MESH,
-        )
-
-    @pl.loop(1, devices)
-    def _(k):
-        loss_copy(k).start()
-
-    write_final(1)
-    write_final(0)
-    rest_of = losses.at[pl.ds(0, devices - 1)]
-    pltpu.make_async_copy(rest_of, rest_of, l_recv).wait()
-    loss_ref[...] = jnp.sum(losses[...], axis=0) / features
+    square = square + gram_product(3)
+    loss_part = redundancy * jnp.sum(square) / (samples * samples) + on_diagonal_all / groups
+    finals[0, 0, 2:3] = jnp.broadcast_to(loss_part, (1, cols))
+    exchange_final(0)
+    for v in (1, 0):
+        table[4 * v : 4 * v + 1] = centers[v]
+        table[4 * v + 1 : 4 * v + 2] = factors[v]
     pltpu.make_async_copy(rest_of, rest_of, l_send).wait()
+    for v in (1, 0):
+        sums = merge_final(v, 3 - v)
+        table[4 * v + 2 : 4 * v + 3] = sums[0] / samples
+        table[4 * v + 3 : 4 * v + 4] = sums[1] / samples
+        if v == 0:
+            table[8:9] = sums[2] / features
     for copy in sent:
         copy.wait_send()
 
@@ -437,10 +447,10 @@
     f32, bf16 = jnp.float32, jnp.bfloat16
     dma = pltpu.SemaphoreType.DMA
     vmem = pl.BlockSpec(memory_space=pltpu.VMEM)
-    loss, grad_a, grad_b = pl.pallas_call(
+    table, dnorm_a, dnorm_b = pl.pallas_call(
         functools.partial(kernel, feats),
         out_shape=(
-            jax.ShapeDtypeStruct((8, 128), f32),
+            jax.ShapeDtypeStruct((16, cols), f32),
             jax.ShapeDtypeStruct((rows, cols), f32),
             jax.ShapeDtypeStruct((rows, cols), f32),
         ),
@@ -459,8 +469,8 @@
             pltpu.VMEM((2, 4, rows, rows), bf16),
             pltpu.VMEM((2, rows, rows), bf16),
             pltpu.VMEM((4, 4, cols), f32),
-            pltpu.VMEM((2, 4, 2, cols), f32),
-            pltpu.VMEM((4 * feats, 8, 128), f32),
+            pltpu.VMEM((2, 4, 4, cols), f32),
+            pltpu.VMEM((feats, 8, 128), f32),
             dma((2, 6)), dma((2, 6)), dma((3,)), dma((3,)),
             dma((8,)), dma((8,)), dma((8, depth - 1)), dma((8, depth - 1)),
             dma((8, depth - 1)), dma((8, depth - 1)), dma((8,)), dma((8,)),
@@ -471,7 +481,13 @@
         ),
         name="twins",
     )(view_a, view_b)
-    return loss[0, 0], grad_a, grad_b
+
+    def grad(dnorm, view, at):
+        center, factor, first, second = (table[at + i] for i in range(4))
+        normed = (view.astype(f32) - center) * factor
+        return (dnorm - first - normed * second) * factor
+
+    return table[8, 0], grad(dnorm_a, view_a, 0), grad(dnorm_b, view_b, 4)
 
 
 def solution(mesh):

time: 78.1 us -> 71.9 us (0.921)
  Pallas kernels: 72.7 us -> 65.1 us
  other arithmetic: 0 us -> 3.41 us
  local copies, waits for them, and re-layouts: 4.56 us -> 2.44 us
    pallas_call x1, Pallas kernels: 72.7 us -> 65.1 us  [local(): pl.pallas_call(functools.partial(kernel, feats), out_shape=(jax.ShapeDtyp...]
    mul x0 -> x1, other arithmetic: none -> 3.41 us  [grad(): return (dnorm - first - normed * second) * factor]
    unnamed x4, local copies, waits for them, and re-layouts: 3.37 us -> 0.01 us
    slice x1 -> x2, local copies, waits for them, and re-layouts: 1.19 us -> 2.44 us  [the longest x1 1.26 us: grad(): center, factor, first, second = (table[at + i] for i in range(4))]
where the time goes in v3:
time: 71.9 us; the launch traced here: 71.6 us
  Pallas kernels  65.1 us (91%)
  other arithmetic  3.41 us (5%)
  local copies, waits for them, and re-layouts  2.44 us (3%)
    pallas_call x1, Pallas kernels, local(): pl.pallas_call(functools.partial(kernel, feats), out_shape=(jax.ShapeDtyp...  65.1 us
    mul x1, other arithmetic, grad(): return (dnorm - first - normed * second) * factor  3.41 us

profile of v3, /device:TPU:0, one launch (start us, length us, event | category | flops | bytes accessed | tf_op | source)
XLA Modules:
  0.0 71.6 jit_solution(15760199201144232145)
XLA Ops:
  0.6 0.0 copy-start.1
  0.6 0.0 copy-start
  0.6 65.1 %twins.1 = (f32[16,1024]{1,0:T(8,128)}, f32[256,1024]{1,0:T(8,128)}, f32[256,1024]{1,0:T(8,128)}) custom-call(bf16[256,1024]{1,0:T(8,128)(2,1)} %view_a.1, bf16[256,1024]{1,0:T(8,128)(2,1)} %view_b.1), custom_call_target="tpu_custom_call" | custom-call | tf_op jit(solution)/shard_map/twins/pallas_call | solution.py:450
  65.7 1.2 %slice.27 = f32[1,1]{1,0:T(1,128)} slice(f32[16,1024]{1,0:T(8,128)} %get-tuple-element.6), slice={[8:9], [0:1]} | slice | bytes 8 | tf_op jit(solution)/shard_map/slice | solution.py:490
  66.9 1.3 %fusion = (f32[1,1024]{1,0:T(1,128)S(1)}, f32[1,1024]{1,0:T(1,128)S(1)}, f32[1,1024]{1,0:T(1,128)S(1)}, f32[1,1024]{1,0:T(1,128)S(1)}, f32[1,1024]{1,0:T(1,128)S...) fusion(f32[16,1024]{1,0:T(8,128)} %get-tuple-element.6), kind=kLoop, calls=%fused_computation.2 | loop fusion | bytes 65536 | tf_op jit(solution)/shard_map/slice | solution.py:486
  68.2 0.0 copy-done.1
  68.2 0.0 copy-done
  68.2 3.4 %subtract_multiply_fusion = (f32[256,1024]{1,0:T(8,128)}, f32[256,1024]{1,0:T(8,128)}) fusion(bf16[256,1024]{1,0:T(8,128)(2,1)S(1)} %copy-done.1, f32[256,1024]{1,0:T(8,128)} %get-tuple-element.8, f32[1024]{0:T(1024)S(1)} %bitcast.10, f32[1024]{0:T(1024)S(1)} %bitcast.11, f32[1024]{0:T(1024)S(1)} %bitcast.12, f32[1024]{0:T(1024)S(1)} %bitcast.9, ...), kind=kLoop, calls=%fused_computation | loop fusion | flops 3670016 | bytes 5275648 | tf_op jit(solution)/shard_map/mul | solution.py:488
Async XLA Ops:
  0.6 67.5 %copy-start.1 = (bf16[256,1024]{1,0:T(8,128)(2,1)S(1)}, bf16[256,1024]{1,0:T(8,128)(2,1)}, u32[]{:S(2)}) copy-start(bf16[256,1024]{1,0:T(8,128)(2,1)} %view_b.1) | copy-start | bytes 1572868
  0.6 67.5 %copy-start = (bf16[256,1024]{1,0:T(8,128)(2,1)S(1)}, bf16[256,1024]{1,0:T(8,128)(2,1)}, u32[]{:S(2)}) copy-start(bf16[256,1024]{1,0:T(8,128)(2,1)} %view_a.1) | copy-start | bytes 1572868

commit v4 on v3

--- a/solution.py
+++ b/solution.py
@@ -440,6 +440,20 @@
         copy.wait_send()
 
 
+def last_step(table, dnorm_a, dnorm_b, view_a, view_b, loss, grad_a, grad_b):
+    rows = view_a.shape[0]
+    for v, (dnorm, view, grad) in enumerate(((dnorm_a, view_a, grad_a), (dnorm_b, view_b, grad_b))):
+        center, factor, first, second = (table[4 * v + i : 4 * v + i + 1] for i in range(4))
+
+        @pl.loop(0, rows // 16)
+        def _(i):
+            r = pl.ds(pl.multiple_of(i * 16, 16), 16)
+            normed = (view[r].astype(jnp.float32) - center) * factor
+            grad[r] = (dnorm[r] - first - normed * second) * factor
+
+    loss[...] = table[8:9, 0:1]
+
+
 def local(feats, view_a, view_b):
     rows, cols = view_a.shape
     half, depth = rows // 2, feats // 2
@@ -477,17 +491,24 @@
             dma((2, 3)), dma((2, 3)), dma, dma,
         ],
         compiler_params=pltpu.CompilerParams(
-            collective_id=0, has_side_effects=True, vmem_limit_bytes=56 * 1024 * 1024
+            collective_id=0, has_side_effects=True, vmem_limit_bytes=20 * 1024 * 1024
         ),
         name="twins",
     )(view_a, view_b)
 
-    def grad(dnorm, view, at):
-        center, factor, first, second = (table[at + i] for i in range(4))
-        normed = (view.astype(f32) - center) * factor
-        return (dnorm - first - normed * second) * factor
-
-    return table[8, 0], grad(dnorm_a, view_a, 0), grad(dnorm_b, view_b, 4)
+    loss, grad_a, grad_b = pl.pallas_call(
+        last_step,
+        out_shape=(
+            jax.ShapeDtypeStruct((1, 1), f32),
+            jax.ShapeDtypeStruct((rows, cols), f32),
+            jax.ShapeDtypeStruct((rows, cols), f32),
+        ),
+        in_specs=[vmem] * 5,
+        out_specs=(vmem, vmem, vmem),
+        compiler_params=pltpu.CompilerParams(vmem_limit_bytes=16 * 1024 * 1024),
+        name="last_step",
+    )(table, dnorm_a, dnorm_b, view_a, view_b)
+    return loss[0, 0], grad_a, grad_b
 
 
 def solution(mesh):

time: 71.9 us -> 67.2 us (0.935)
  other arithmetic: 3.41 us -> 0 us
  Pallas kernels: 65.1 us -> 64.3 us
    mul x1 -> x0, other arithmetic: 3.41 us -> none  [grad(): return (dnorm - first - normed * second) * factor]
    pallas_call x1, Pallas kernels: 65.1 us -> 62.2 us  [local(): pl.pallas_call(functools.partial(kernel, feats), out_shape=(jax.ShapeDtyp...]
    slice x2 -> x0, local copies, waits for them, and re-layouts: 2.44 us -> none  [the longest x1 1.26 us: grad(): center, factor, first, second = (table[at + i] for i in range(4))]
    pallas_call x0 -> x1, Pallas kernels: none -> 2.1 us  [local(): pl.pallas_call(last_step, out_shape=(jax.ShapeDtypeStruct((1, 1), f32), j...]
    unnamed x4, local copies, waits for them, and re-layouts: 0.01 us -> 2.08 us
where the time goes in v4:
time: 67.2 us; the launch traced here: 67 us
  Pallas kernels  64.3 us (96%)
  local copies, waits for them, and re-layouts  2.08 us (3%)
    pallas_call x1, Pallas kernels, local(): pl.pallas_call(functools.partial(kernel, feats), out_shape=(jax.ShapeDtyp...  62.2 us
    pallas_call x1, Pallas kernels, local(): pl.pallas_call(last_step, out_shape=(jax.ShapeDtypeStruct((1, 1), f32), j...  2.1 us
    unnamed x4, local copies, waits for them, and re-layouts  2.08 us

profile of v4, /device:TPU:0, one launch (start us, length us, event | category | flops | bytes accessed | tf_op | source)
XLA Modules:
  0.0 67.0 jit_solution(4988830031907363645)
XLA Ops:
  0.6 0.0 copy-start
  0.6 1.0 %copy-done = bf16[256,1024]{1,0:T(8,128)(2,1)S(1)} copy-done((bf16[256,1024]{1,0:T(8,128)(2,1)S(1)}, bf16[256,1024]{1,0:T(8,128)(2,1)}, u32[]{:S(2)}) %copy-start) | copy-done | bytes 524312
  1.7 0.0 copy-start.1
  1.7 1.0 %copy-done.1 = bf16[256,1024]{1,0:T(8,128)(2,1)S(1)} copy-done((bf16[256,1024]{1,0:T(8,128)(2,1)S(1)}, bf16[256,1024]{1,0:T(8,128)(2,1)}, u32[]{:S(2)}) %copy-start.1) | copy-done | bytes 524312
  2.7 62.2 %twins.1 = (f32[16,1024]{1,0:T(8,128)S(1)}, f32[256,1024]{1,0:T(8,128)S(1)}, f32[256,1024]{1,0:T(8,128)S(1)}) custom-call(bf16[256,1024]{1,0:T(8,128)(2,1)S(1)} %copy-done, bf16[256,1024]{1,0:T(8,128)(2,1)S(1)} %copy-done.1), custom_call_target="tpu_custom_call" | custom-call | tf_op jit(solution)/shard_map/twins/pallas_call | solution.py:464
  64.9 2.1 %last_step.1 = (f32[1,1]{1,0:T(1,128)}, f32[256,1024]{1,0:T(8,128)}, f32[256,1024]{1,0:T(8,128)}) custom-call(f32[16,1024]{1,0:T(8,128)S(1)} %get-tuple-element.9.table, f32[256,1024]{1,0:T(8,128)S(1)} %get-tuple-element.10.dnorm_a, f32[256,1024]{1,0:T(8,128)S(1)} %get-tuple-element.11.dnorm_b, bf16[256,1024]{1,0:T(8,128)(2,1)S(1)} %copy-done, ...), custom_call_target="tpu_custom_call" | custom-call | tf_op jit(solution)/shard_map/last_step/pallas_call | solution.py:499
Async XLA Ops:
  0.6 1.0 %copy-start = (bf16[256,1024]{1,0:T(8,128)(2,1)S(1)}, bf16[256,1024]{1,0:T(8,128)(2,1)}, u32[]{:S(2)}) copy-start(bf16[256,1024]{1,0:T(8,128)(2,1)} %view_a.3) | copy-start | bytes 1572868
  1.7 1.0 %copy-start.1 = (bf16[256,1024]{1,0:T(8,128)(2,1)S(1)}, bf16[256,1024]{1,0:T(8,128)(2,1)}, u32[]{:S(2)}) copy-start(bf16[256,1024]{1,0:T(8,128)(2,1)} %view_b.3) | copy-start | bytes 1572868

commit v5 on v4

--- a/solution.py
+++ b/solution.py
@@ -85,12 +85,12 @@
         pieces = term(pl.ds(pl.multiple_of(i * step, step), step))
         return tuple(c + fold(p) for c, p in zip(carry, pieces))
 
-    sums = lax.fori_loop(0, rows // step, body, (zero,) * count)
+    sums = lax.fori_loop(0, rows // step, body, (zero,) * count, unroll=4)
     return tuple(jnp.sum(s, axis=0, keepdims=True) for s in sums)
 
 
 def kernel(
-    feats, view_a, view_b, table, grad_a, grad_b,
+    feats, source_a, source_b, table, grad_a, grad_b, view_a, view_b, load,
     raw, low, part, pair_in, sum0, in0, sum1, in1, gram0, gram, rest0,
     stats, finals, losses,
     g_send, g_recv, s_send, s_recv, p_send, p_recv, z_send, z_recv,
@@ -98,6 +98,12 @@
 ):
     views, grads = (view_a, view_b), (grad_a, grad_b)
     rows, cols = view_a.shape
+    loads = [
+        pltpu.make_async_copy(source_a, view_a, load.at[0]),
+        pltpu.make_async_copy(source_b, view_b, load.at[1]),
+    ]
+    for copy in loads:
+        copy.start()
     half = rows // 2
     groups = 4
     depth = feats // 2
@@ -156,8 +162,10 @@
                 {"batch": peers[1 - link]},
             )
 
+    loads[0].wait()
     own(0, 0, 0)
     own(0, 1, 1)
+    loads[1].wait()
 
     means = column_sums(
         rows, cols, 2,
@@ -201,7 +209,7 @@
         source = views[v] if slot == 0 else raw.at[v, slot - 1]
         count, base = (rows, 0) if part_of is None else (half, part_of * half)
 
-        @pl.loop(0, count // 16)
+        @pl.loop(0, count // 16, unroll=4)
         def _(i):
             r = pl.ds(pl.multiple_of(base + i * 16, 16), 16)
             values = source[r].astype(jnp.float32)
@@ -445,7 +453,7 @@
     for v, (dnorm, view, grad) in enumerate(((dnorm_a, view_a, grad_a), (dnorm_b, view_b, grad_b))):
         center, factor, first, second = (table[4 * v + i : 4 * v + i + 1] for i in range(4))
 
-        @pl.loop(0, rows // 16)
+        @pl.loop(0, rows // 16, unroll=4)
         def _(i):
             r = pl.ds(pl.multiple_of(i * 16, 16), 16)
             normed = (view[r].astype(jnp.float32) - center) * factor
@@ -468,9 +476,12 @@
             jax.ShapeDtypeStruct((rows, cols), f32),
             jax.ShapeDtypeStruct((rows, cols), f32),
         ),
-        in_specs=[vmem, vmem],
+        in_specs=[pl.BlockSpec(memory_space=pltpu.HBM)] * 2,
         out_specs=(vmem, vmem, vmem),
         scratch_shapes=[
+            pltpu.VMEM((rows, cols), bf16),
+            pltpu.VMEM((rows, cols), bf16),
+            dma((2,)),
             pltpu.VMEM((2, 3, rows, cols), bf16),
             pltpu.VMEM((2, 4, rows, cols), bf16),
             pltpu.VMEM((8, rows, rows), f32),

time: 67.2 us -> 68.1 us (1.013)
  Pallas kernels: 64.3 us -> 65.1 us
    pallas_call x1, Pallas kernels: 62.2 us -> 63.2 us  [local(): pl.pallas_call(functools.partial(kernel, feats), out_shape=(jax.ShapeDtyp...]
where the time goes in v5:
time: 68.1 us; the launch traced here: 67.9 us
  Pallas kernels  65.1 us (96%)
  local copies, waits for them, and re-layouts  2.08 us (3%)
    pallas_call x1, Pallas kernels, local(): pl.pallas_call(functools.partial(kernel, feats), out_shape=(jax.ShapeDtyp...  63.2 us
    unnamed x4, local copies, waits for them, and re-layouts  2.08 us
    pallas_call x1, Pallas kernels, local(): pl.pallas_call(last_step, out_shape=(jax.ShapeDtypeStruct((1, 1), f32), j...  1.92 us

profile of v5, /device:TPU:0, one launch (start us, length us, event | category | flops | bytes accessed | tf_op | source)
XLA Modules:
  0.0 67.9 jit_solution(18274492139544105711)
XLA Ops:
  0.6 0.0 copy-start
  0.6 1.0 %copy-done = bf16[256,1024]{1,0:T(8,128)(2,1)S(1)} copy-done((bf16[256,1024]{1,0:T(8,128)(2,1)S(1)}, bf16[256,1024]{1,0:T(8,128)(2,1)}, u32[]{:S(2)}) %copy-start) | copy-done | bytes 524312
  1.7 0.0 copy-start.1
  1.7 1.0 %copy-done.1 = bf16[256,1024]{1,0:T(8,128)(2,1)S(1)} copy-done((bf16[256,1024]{1,0:T(8,128)(2,1)S(1)}, bf16[256,1024]{1,0:T(8,128)(2,1)}, u32[]{:S(2)}) %copy-start.1) | copy-done | bytes 524312
  2.7 63.2 %twins.1 = (f32[16,1024]{1,0:T(8,128)S(1)}, f32[256,1024]{1,0:T(8,128)S(1)}, f32[256,1024]{1,0:T(8,128)S(1)}) custom-call(bf16[256,1024]{1,0:T(8,128)(2,1)S(1)} %copy-done, bf16[256,1024]{1,0:T(8,128)(2,1)S(1)} %copy-done.1), custom_call_target="tpu_custom_call" | custom-call | tf_op jit(solution)/shard_map/twins/pallas_call | solution.py:472
  65.9 1.9 %last_step.1 = (f32[1,1]{1,0:T(1,128)}, f32[256,1024]{1,0:T(8,128)}, f32[256,1024]{1,0:T(8,128)}) custom-call(f32[16,1024]{1,0:T(8,128)S(1)} %get-tuple-element.9.table, f32[256,1024]{1,0:T(8,128)S(1)} %get-tuple-element.10.dnorm_a, f32[256,1024]{1,0:T(8,128)S(1)} %get-tuple-element.11.dnorm_b, bf16[256,1024]{1,0:T(8,128)(2,1)S(1)} %copy-done, ...), custom_call_target="tpu_custom_call" | custom-call | tf_op jit(solution)/shard_map/last_step/pallas_call | solution.py:510
Async XLA Ops:
  0.6 1.0 %copy-start = (bf16[256,1024]{1,0:T(8,128)(2,1)S(1)}, bf16[256,1024]{1,0:T(8,128)(2,1)}, u32[]{:S(2)}) copy-start(bf16[256,1024]{1,0:T(8,128)(2,1)} %view_a.1) | copy-start | bytes 1572868
  1.7 1.0 %copy-start.1 = (bf16[256,1024]{1,0:T(8,128)(2,1)S(1)}, bf16[256,1024]{1,0:T(8,128)(2,1)}, u32[]{:S(2)}) copy-start(bf16[256,1024]{1,0:T(8,128)(2,1)} %view_b.1) | copy-start | bytes 1572868
